TPU v7x, 128 devices: a whole 4x4x4 slice. The times are simulated.
128 devices in a mesh: fsdp: 64 (over x_lo, y, z, core), grp: 2 (over x_hi).
Axes of the slice: x: 4 (x_hi: 2, x_lo: 2; x = x_hi * 2 + x_lo), y: 4, z: 4, core: 2. Of those that a mesh axis runs over, the one named last changes fastest.
Arguments:
- hidden: bfloat16 [32768, 3072], P('fsdp', 'grp'), may hold values from -16 to 16
- queries: bfloat16 [32768, 1536], P('fsdp', 'grp'), may hold values from -6 to 6
- attn_keys: bfloat16 [32768, 1536], P('fsdp', 'grp'), may hold values from -6 to 6
- w_value: bfloat16 [1536, 3072], P('fsdp', 'grp'), may hold values from -1 to 1
- w_out: bfloat16 [1536, 3072], P('fsdp', 'grp'), may hold values from -1 to 1
- alpha: float32 [3072], P('grp'), may hold values from 0.05 to 0.5
- out_grad: bfloat16 [32768, 3072], P('fsdp', 'grp'), may hold values from -6 to 6
Outputs:
- new_hidden: bfloat16 [32768, 3072], P('fsdp', 'grp')
- grad_hidden: bfloat16 [32768, 3072], P('fsdp', 'grp')
- grad_queries: bfloat16 [32768, 1536], P('fsdp', 'grp')
- grad_keys: bfloat16 [32768, 1536], P('fsdp', 'grp')
- grad_w_value: float32 [1536, 3072], P('fsdp', 'grp')
- grad_w_out: float32 [1536, 3072], P('fsdp', 'grp')
All inputs are finite; a program needn't handle non-finite values.
Results may differ from a plain program's by a relative error of at most 0.012.
The roundings to bfloat16 on the way count: a program that leaves them out, or rounds other values in their place, can miss the bound.
Values may be sent and summed in bfloat16 or wider, within the bound.
No kernel may reach another device: no remote copies, remote signals or barrier semaphores. Data moves between devices by JAX's collectives and lax.ppermute only.
A program may use at most 192 MiB of HBM per device.

v0:
```python
import jax
import jax.numpy as jnp
from jax import lax
from jax.sharding import Mesh
from jax.sharding import PartitionSpec as P

D = 3072
HS = 128
FSDP = ("fsdp_0", "fsdp_1", "fsdp_2", "fsdp_3")
EPS = 1e-06


def from_everyone(value, axis):
    count = lax.axis_size(axis)
    return lax.all_to_all(
        jnp.broadcast_to(value[None], (count, *value.shape)), axis, 0, 0, tiled=True
    )


def of_everyone(value, axis):
    everything = from_everyone(value, axis)
    return jnp.sum(everything, axis=0)


def packed_total(arrays, axis):
    ends = [0]
    for a in arrays:
        ends.append(ends[-1] + a.size)
    subtotal = of_everyone(jnp.concatenate([a.ravel() for a in arrays]), axis)
    return tuple((subtotal[b:e].reshape(a.shape) for a, b, e in zip(arrays, ends, ends[1:])))


def sent_together(arrays, axis, dim, along):
    ends, at = ([], 0)
    for a in arrays[:-1]:
        at += a.shape[along]
        ends.append(at)
    both = jnp.concatenate(arrays, axis=along)
    return tuple(jnp.split(lax.all_gather(both, axis, axis=dim, tiled=True), ends, axis=along))


def cut_along(value, dim, count):
    before, after = (value.shape[:dim], value.shape[dim + 1 :])
    return jnp.moveaxis(value.reshape(*before, count, -1, *after), dim, 0)


def summed_on_arrival(value, axis, dim):
    tiles = cut_along(value, dim, lax.axis_size(axis))
    arrived = lax.all_to_all(tiles, axis, split_axis=0, concat_axis=0, tiled=True)
    return arrived.sum(axis=0)


def laid_out(tiles, dim):
    tiles = jnp.moveaxis(tiles, 0, dim)
    dims = tiles.shape
    return tiles.reshape(*dims[:dim], dims[dim] * dims[dim + 1], *dims[dim + 2 :])


def collect(value, axis, dim):
    return laid_out(from_everyone(value, axis), dim)


def summed_rows(value, chips, core, dim):
    sizes = (lax.axis_size(chips), lax.axis_size(core))
    tiles = cut_along(value, dim, sizes[0] * sizes[1])
    inside = tiles.shape[1:]
    tiles = tiles.reshape(*sizes, *inside).swapaxes(0, 1).reshape(-1, *inside)
    tiles = lax.psum_scatter(tiles, core, scatter_dimension=0, tiled=True)
    return lax.psum_scatter(tiles, chips, scatter_dimension=0, tiled=True)[0]


def contract_last(left, right):
    return lax.dot_general(
        left, right, (((1,), (1,)), ((), ())), preferred_element_type=jnp.float32
    )


def contract_first(left, right):
    return lax.dot_general(
        left, right, (((0,), (0,)), ((), ())), preferred_element_type=jnp.float32
    )


def causal_probs(query_head, key_head):
    length = query_head.shape[0]
    score_scale = query_head.shape[1] ** (-0.5)
    scores = contract_last(query_head, key_head) * score_scale
    row_pos = lax.broadcasted_iota(jnp.int32, (length, length), 0)
    col_pos = lax.broadcasted_iota(jnp.int32, (length, length), 1)
    scores = jnp.where(row_pos >= col_pos, scores, -1e30)
    row_peak = jnp.max(scores, axis=1, keepdims=True)
    exp_terms = jnp.exp(scores - row_peak)
    return exp_terms / jnp.sum(exp_terms, axis=1, keepdims=True)


def head_forward(items):
    query_head, key_head, value_head = items
    attn_prob = causal_probs(query_head, key_head)
    return jnp.dot(
        attn_prob.astype(jnp.bfloat16), value_head, preferred_element_type=jnp.float32
    ).astype(jnp.bfloat16)


def head_backward(items):
    query_head, key_head, value_head, grad_head = items
    score_scale = query_head.shape[1] ** (-0.5)
    attn_prob = causal_probs(query_head, key_head)
    prob_half = attn_prob.astype(jnp.bfloat16)
    grad_prob = contract_last(grad_head, value_head)
    row_delta = jnp.sum(attn_prob * grad_prob, axis=1, keepdims=True)
    grad_score = (attn_prob * (grad_prob - row_delta)).astype(jnp.bfloat16)
    grad_query = (
        jnp.dot(grad_score, key_head, preferred_element_type=jnp.float32) * score_scale
    ).astype(jnp.bfloat16)
    grad_key = (contract_first(grad_score, query_head) * score_scale).astype(jnp.bfloat16)
    grad_value = contract_first(prob_half, grad_head).astype(jnp.bfloat16)
    return (grad_query, grad_key, grad_value)


def split_heads(block):
    return block.reshape(block.shape[0], -1, HS).transpose(1, 0, 2)


def join_heads(stacked):
    return stacked.transpose(1, 0, 2).reshape(stacked.shape[1], -1)


def shards(hidden, queries, attn_keys, w_value, w_out, alpha, out_grad):
    half_width = hidden.shape[1]
    value_rows = w_value.astype(jnp.float32)
    out_rows = w_out.astype(jnp.float32)
    row_sums = packed_total(
        (jnp.sum(value_rows * value_rows, axis=1), jnp.sum(out_rows * out_rows, axis=1)), "grp"
    )
    norm_v = jnp.sqrt(row_sums[0] + EPS)[:, None]
    norm_o = jnp.sqrt(row_sums[1] + EPS)[:, None]
    unit_v = value_rows / norm_v
    unit_o = out_rows / norm_o
    weight_v, weight_o = sent_together(
        (unit_v.astype(jnp.bfloat16), unit_o.astype(jnp.bfloat16)), FSDP, 0, 1
    )
    value_parts = contract_last(hidden, weight_v)
    values_mine = summed_on_arrival(value_parts, "grp", 1).astype(jnp.bfloat16)
    q_heads = split_heads(queries)
    k_heads = split_heads(attn_keys)
    v_heads = split_heads(values_mine)
    attn_mine = join_heads(lax.map(head_forward, (q_heads, k_heads, v_heads)))
    attn_all = collect(attn_mine, "grp", 1)
    proj = jnp.dot(attn_all, weight_o, preferred_element_type=jnp.float32)
    hidden_f = hidden.astype(jnp.float32)
    keep_rate = 1.0 - alpha
    moments = packed_total(
        (
            jnp.sum(proj * proj, axis=1),
            jnp.sum(keep_rate * keep_rate * hidden_f * hidden_f, axis=1),
            jnp.sum(keep_rate * alpha * hidden_f * proj, axis=1),
            jnp.sum(alpha * alpha * proj * proj, axis=1),
        ),
        "grp",
    )
    proj_rs = lax.rsqrt(moments[0] / D + EPS)[:, None]
    cross_sum = moments[2][:, None]
    alpha_sum = moments[3][:, None]
    mix_mean = (moments[1][:, None] + 2.0 * proj_rs * cross_sum + proj_rs * proj_rs * alpha_sum) / D
    mix_rs = lax.rsqrt(mix_mean + EPS)
    mixed = hidden_f + alpha * (proj * proj_rs - hidden_f)
    new_hidden = (mixed * mix_rs).astype(jnp.bfloat16)
    grad_out = out_grad.astype(jnp.float32)
    grad_sums = packed_total(
        (
            jnp.sum(grad_out * keep_rate * hidden_f, axis=1),
            jnp.sum(grad_out * alpha * proj, axis=1),
        ),
        "grp",
    )
    grad_mean = (grad_sums[0][:, None] + proj_rs * grad_sums[1][:, None]) / D
    grad_mix = mix_rs * (grad_out - mixed * mix_rs * mix_rs * grad_mean)
    grad_pn = grad_mix * alpha
    proj_mean = (
        mix_rs * grad_sums[1][:, None]
        - mix_rs * mix_rs * mix_rs * grad_mean * (cross_sum + proj_rs * alpha_sum)
    ) / D
    grad_res = grad_mix * keep_rate
    grad_proj = proj_rs * (grad_pn - proj * proj_rs * proj_rs * proj_mean)
    grad_proj_b = grad_proj.astype(jnp.bfloat16)
    grad_attn_parts = contract_last(grad_proj_b, weight_o)
    grad_attn = summed_on_arrival(grad_attn_parts, "grp", 1).astype(jnp.bfloat16)
    grad_q, grad_k, grad_v = lax.map(
        head_backward, (q_heads, k_heads, v_heads, split_heads(grad_attn))
    )
    grad_values = collect(join_heads(grad_v), "grp", 1)
    grad_hidden = (
        grad_res + jnp.dot(grad_values, weight_v, preferred_element_type=jnp.float32)
    ).astype(jnp.bfloat16)
    owned = summed_rows(
        jnp.concatenate(
            (contract_first(grad_values, hidden), contract_first(attn_all, grad_proj_b)), axis=1
        ),
        ("fsdp_0", "fsdp_1", "fsdp_2"),
        "fsdp_3",
        0,
    )
    gw_v_own = owned[:, :half_width]
    gw_o_own = owned[:, half_width:]
    row_dot = packed_total(
        (jnp.sum(gw_v_own * unit_v, axis=1), jnp.sum(gw_o_own * unit_o, axis=1)), "grp"
    )
    grad_w_value = (gw_v_own - unit_v * row_dot[0][:, None]) / norm_v
    grad_w_out = (gw_o_own - unit_o * row_dot[1][:, None]) / norm_o
    return (
        new_hidden,
        grad_hidden,
        join_heads(grad_q),
        join_heads(grad_k),
        grad_w_value,
        grad_w_out,
    )


def solution(mesh):
    torus = Mesh(
        mesh.devices.reshape(2, 4, 4, 2, mesh.shape["grp"]),
        ("fsdp_0", "fsdp_1", "fsdp_2", "fsdp_3", "grp"),
    )
    placed = (
        P(FSDP, "grp"),
        P(FSDP, "grp"),
        P(FSDP, "grp"),
        P(FSDP, "grp"),
        P(FSDP, "grp"),
        P("grp"),
        P(FSDP, "grp"),
    )
    return jax.shard_map(
        shards,
        mesh=torus,
        in_specs=placed,
        out_specs=(
            P(FSDP, "grp"),
            P(FSDP, "grp"),
            P(FSDP, "grp"),
            P(FSDP, "grp"),
            P(FSDP, "grp"),
            P(FSDP, "grp"),
        ),
        check_vma=False,
    )
```

profile of v0, /device:TPU:6, one launch (start us, length us, event | category | flops | bytes accessed | tf_op | source)
XLA Modules:
  0.0 652.1 jit_solution(13862439651871433867)
XLA Ops:
  8.4 6.3 all_to_all.44
  17.4 114.7 %all-gather.2.cloned.1.call-done = bf16[1536,3072]{1,0:T(8,128)(2,1)} async-done(((bf16[24,3072]{1,0:T(8,128)(2,1)}), bf16[1536,3072]{1,0:T(8,128)(2,1)}) %all-gather.2.cloned.1.call-update) | async-done | bytes 9437200 | tf_op jit(solution)/shard_map/all_gather | solution.py:39
  132.1 7.2 %fusion.47 = f32[1536,512]{1,0:T(8,128)} fusion(bf16[512,1536]{1,0:T(8,128)(2,1)} %param.11, bf16[1536,3072]{1,0:T(8,128)(2,1)} %all-gather.2.cloned.1.call-done), kind=kOutput, calls=%fused_computation.74 | convolution fusion | flops 2415919104 | bytes 9437184 | tf_op jit(solution)/shard_map/dot_general | solution.py:73
  139.3 4.8 all-to-all-start.1
  144.1 2.3 copy.89
  146.4 2.3 copy.92
  148.7 2.3 copy.90
  151.0 2.3 copy.93
  153.3 25.8 %all-to-all-done.1 = f32[2,512,768]{1,2,0:T(8,128)S(1)} async-done(((f32[2,512,768]{1,2,0:T(8,128)}), f32[2,512,768]{1,2,0:T(8,128)S(1)}, u32[]{:S(2)}, u32[]{:S(2)}) %all-to-all-start.1) | async-done | bytes 3145760 | tf_op jit(solution)/shard_map/all_to_all | solution.py:49
  182.1 12.2 %while.24 = (s32[]{:T(128)}, bf16[6,512,128]{1,2,0:T(8,128)(2,1)S(1)}, bf16[6,512,128]{2,1,0:T(8,128)(2,1)}, bf16[6,512,128]{2,1,0:T(8,128)(2,1)}, bf16[6,512,128]{2,1,0:T(8,128)(2,1)S(1)}, /*index=5*/s32[]{:T(128)}) while((s32[]{:T(128)}, bf16[6,512,128]{1,2,0:T(8,128)(2,1)S(1)}, bf16[6,512,128]{2,1,0:T(8,128)(2,1)}, ...), condition=%wide.region_7.8_spmd, body=%wide.region_4.7_spmd.sunk | while | flops 136641536 | bytes 4205653 | solution.py:147
  195.7 6.9 %all-to-all-start.2 = ((bf16[2,512,768]{1,2,0:T(8,128)(2,1)}), bf16[2,512,768]{1,2,0:T(8,128)(2,1)S(1)}, u32[]{:S(2)}, u32[]{:S(2)}) async-start(bf16[2,512,768]{1,2,0:T(8,128)(2,1)} %broadcast_in_dim.40), calls=%async_computation.2 | async-start | bytes 3145728 | tf_op jit(solution)/shard_map/all_to_all | solution.py:15
  202.6 17.3 %all-to-all-done.2 = bf16[2,512,768]{1,2,0:T(8,128)(2,1)S(1)} async-done(((bf16[2,512,768]{1,2,0:T(8,128)(2,1)}), bf16[2,512,768]{1,2,0:T(8,128)(2,1)S(1)}, u32[]{:S(2)}, u32[]{:S(2)}) %all-to-all-start.2) | async-done | bytes 1572896 | tf_op jit(solution)/shard_map/all_to_all | solution.py:15
  221.0 8.4 %fusion.54 = (f32[512]{0:T(512)S(1)}, f32[512]{0:T(512)S(1)}, f32[512]{0:T(512)S(1)}, f32[512]{0:T(512)S(1)}, f32[512]{0:T(512)S(1)}, /*index=5*/f32[512]{0:T(512)S(1)}, f32[512,1536]{1,0:T(8,128)S(1)}) fusion(bf16[512,1536]{1,0:T(8,128)(2,1)} %param.17, f32[1536]{0:T(1024)S(1)} %copy-done.10, f32[1536]{0:T(1024)S(1)} %get-tuple-element.225, ...), kind=kOutput, calls=%fused_computation.79 | convolution fusion | flops 2430858240 | bytes 12625920 | tf_op jit(solution)/shard_map/dot_general | solution.py:149
  230.1 6.5 all-to-all-start.4
  239.0 6.7 %all-to-all-start.3 = ((f32[2,1,2048]{2,1,0:T(1,128)}), f32[2,1,2048]{2,1,0:T(1,128)S(1)}, u32[]{:S(2)}, u32[]{:S(2)}) async-start(f32[2,1,2048]{2,1,0:T(1,128)} %broadcast_in_dim.41), calls=%async_computation.3 | async-start | bytes 32768 | tf_op jit(solution)/shard_map/all_to_all | solution.py:15
  247.8 4.4 multiply_convert_fusion.1
  252.2 5.1 fusion.41
  257.5 36.9 %all_to_all.45 = f32[2,512,768]{2,1,0:T(8,128)S(1)} all-to-all(f32[2,512,768]{2,1,0:T(8,128)S(1)} %bitcast.142), channel_id=1, replica_groups=mesh['fsdp_0'=2,'fsdp_1'=4,'fsdp_2'=4,'fsdp_3'=2,'grp'=2] {'grp'}, dimensions={0} | all-to-all | bytes 6291456 | tf_op jit(solution)/shard_map/all_to_all | solution.py:49
  295.8 2.3 copy.100
  299.2 47.0 %while.25 = (s32[]{:T(128)}, bf16[6,512,128]{1,2,0:T(8,128)(2,1)S(1)}, bf16[6,512,128]{1,2,0:T(8,128)(2,1)S(1)}, bf16[6,512,128]{1,2,0:T(8,128)(2,1)}, bf16[6,51...) while((s32[]{:T(128)}, ...), condition=%wide.region_21.22_spmd, body=%wide.region_17.21_spmd.sunk | while | flops 340589056 | bytes 11821177 | solution.py:188
  346.2 2.4 broadcast_in_dim.47
  348.6 7.8 %all-to-all-start.6 = ((bf16[2,512,768]{1,2,0:T(8,128)(2,1)}), bf16[2,512,768]{1,2,0:T(8,128)(2,1)}, u32[]{:S(2)}, u32[]{:S(2)}) async-start(bf16[2,512,768]{1,2,0:T(8,128)(2,1)} %broadcast_in_dim.47), calls=%async_computation.6 | async-start | bytes 3145728 | tf_op jit(solution)/shard_map/all_to_all | solution.py:15
  356.4 8.3 %fusion.86 = f32[1536,1536]{0,1:T(8,128)} fusion(bf16[512,1536]{0,1:T(8,128)(2,1)} %bitcast.153, bf16[512,1536]{1,0:T(8,128)(2,1)} %copy-done.4), kind=kOutput, calls=%fused_computation.133 | convolution fusion | flops 2415919104 | bytes 12582912 | tf_op jit(solution)/shard_map/dot_general | solution.py:79
  364.7 5.1 all-to-all-done.6
  369.8 4.2 fusion.85
  374.0 7.2 %pad_maximum_fusion = f32[1536,3072]{0,1:T(8,128)} fusion(f32[1536,1536]{0,1:T(8,128)S(1)} %copy-done, f32[1536,1536]{0,1:T(8,128)S(1)} %fusion.85), kind=kLoop, calls=%fused_computation.57 | loop fusion | flops 4718592 | bytes 37748736 | tf_op jit(solution)/shard_map/concatenate | solution.py:196
  381.2 18.7 %copy.108 = f32[1536,3072]{1,0:T(8,128)} copy(f32[1536,3072]{0,1:T(8,128)} %pad_maximum_fusion) | data formatting | bytes 37748736 | tf_op jit(solution)/shard_map/concatenate | solution.py:196
  399.9 12.8 %copy.109 = f32[2,32,24,3072]{3,2,1,0:T(8,128)} copy(f32[2,32,24,3072]{3,2,0,1:T(8,128)} %bitcast.141) | data formatting | bytes 37748736 | tf_op jit(solution)/shard_map/transpose | solution.py:67
  412.8 29.1 %reduce-scatter.3.cloned.1.call-done = f32[32,24,3072]{2,1,0:T(8,128)} async-done(((f32[64,24,3072]{2,1,0:T(8,128)}), f32[32,24,3072]{2,1,0:T(8,128)}) %reduce-scatter.3.cloned.1.call-update) | async-done | bytes 9437200 | tf_op jit(solution)/shard_map/reduce_scatter | solution.py:68
  444.3 184.6 %reduce-scatter.5.cloned.1.call-done = f32[1,24,3072]{2,1,0:T(8,128)} async-done(((f32[32,24,3072]{2,1,0:T(8,128)}), f32[1,24,3072]{2,1,0:T(8,128)}) %reduce-scatter.5.cloned.1.call-update) | async-done | bytes 294928 | tf_op jit(solution)/shard_map/reduce_scatter | solution.py:69
  630.8 4.8 all-to-all-start.7
  635.6 9.1 %fusion.62 = bf16[512,1536]{1,0:T(8,128)(2,1)} fusion(bf16[512,1536]{0,1:T(8,128)(2,1)} %bitcast.34, bf16[1536,3072]{1,0:T(8,128)(2,1)} %all-gather.2.cloned.1.call-done, bf16[512,1536]{1,0:T(8,128)(2,1)S(1)} %copy-done.2, f32[512]{0:T(512)S(1)} %get-tuple-element.211, f32[1536]{0:T(1024)S(1)} %get-tuple-element.228, f32[512]{0:T(512)S(1)} %get-tuple-element.226, ...), kind=kOutput, calls=%fused_computation.90 | convolution fusion | flops 2426929152 | bytes 14174208 | tf_op jit(solution)/shard_map/dot_general | solution.py:193
  (166 shorter events, 81.0 us)
Async XLA Ops:
  7.2 125.0 %all-gather.2.cloned.1.call-start = ((), (), s32[]{:S(2)}) async-start(), calls=%async_computation.10 | async-start | bytes 9584640 | tf_op jit(solution)/shard_map/all_gather | solution.py:39
  139.3 39.8 %all-to-all-start.1 = ((f32[2,512,768]{1,2,0:T(8,128)}), f32[2,512,768]{1,2,0:T(8,128)S(1)}, u32[]{:S(2)}, u32[]{:S(2)}) async-start(f32[2,512,768]{1,2,0:T(8,128)} %bitcast.143), calls=%async_computation.1 | async-start | bytes 6291456 | tf_op jit(solution)/shard_map/all_to_all | solution.py:49
  194.2 1.4 copy-start.9
  194.3 8.3 %copy-start.10 = (f32[1536]{0:T(1024)S(1)}, f32[1536]{0:T(1024)}, u32[]{:S(2)}) copy-start(f32[1536]{0:T(1024)} %param.16) | copy-start | bytes 18436
  195.7 24.2 %all-to-all-start.2 = ((bf16[2,512,768]{1,2,0:T(8,128)(2,1)}), bf16[2,512,768]{1,2,0:T(8,128)(2,1)S(1)}, u32[]{:S(2)}, u32[]{:S(2)}) async-start(bf16[2,512,768]{1,2,0:T(8,128)(2,1)} %broadcast_in_dim.40), calls=%async_computation.2 | async-start | bytes 3145728 | tf_op jit(solution)/shard_map/all_to_all | solution.py:15
  219.9 1.1 copy-start.5
  229.4 22.7 %copy-start.1 = (f32[512,1536]{1,0:T(8,128)}, f32[512,1536]{1,0:T(8,128)S(1)}, u32[]{:S(2)}) copy-start(f32[512,1536]{1,0:T(8,128)S(1)} %get-tuple-element.234) | copy-start | bytes 9437188
  230.1 8.3 %all-to-all-start.4 = ((f32[2,1,1024]{2,1,0:T(1,128)}), f32[2,1,1024]{2,1,0:T(1,128)S(1)}, u32[]{:S(2)}, u32[]{:S(2)}) async-start(f32[2,1,1024]{2,1,0:T(1,128)} %broadcast_in_dim.42), calls=%async_computation.4 | async-start | bytes 16384 | tf_op jit(solution)/shard_map/all_to_all | solution.py:15
  239.0 8.8 %all-to-all-start.3 = ((f32[2,1,2048]{2,1,0:T(1,128)}), f32[2,1,2048]{2,1,0:T(1,128)S(1)}, u32[]{:S(2)}, u32[]{:S(2)}) async-start(f32[2,1,2048]{2,1,0:T(1,128)} %broadcast_in_dim.41), calls=%async_computation.3 | async-start | bytes 32768 | tf_op jit(solution)/shard_map/all_to_all | solution.py:15
  252.2 5.1 copy-start.4
  348.6 21.2 %all-to-all-start.6 = ((bf16[2,512,768]{1,2,0:T(8,128)(2,1)}), bf16[2,512,768]{1,2,0:T(8,128)(2,1)}, u32[]{:S(2)}, u32[]{:S(2)}) async-start(bf16[2,512,768]{1,2,0:T(8,128)(2,1)} %broadcast_in_dim.47), calls=%async_computation.6 | async-start | bytes 3145728 | tf_op jit(solution)/shard_map/all_to_all | solution.py:15
  356.4 13.4 %copy-start.3 = (bf16[512,1536]{1,0:T(8,128)(2,1)S(1)}, bf16[512,1536]{1,0:T(8,128)(2,1)}, u32[]{:S(2)}) copy-start(bf16[512,1536]{1,0:T(8,128)(2,1)} %param.11) | copy-start | bytes 4718596
  356.4 85.5 %reduce-scatter.3.cloned.1.call-start = ((), (), s32[]{:S(2)}) async-start(), calls=%async_computation.11 | async-start | bytes 28311552 | tf_op jit(solution)/shard_map/reduce_scatter | solution.py:68
  369.8 4.3 copy-start
  412.8 216.1 %reduce-scatter.5.cloned.1.call-start = ((), (), s32[]{:S(2)}) async-start(), calls=%async_computation.12 | async-start | bytes 9732096 | tf_op jit(solution)/shard_map/reduce_scatter | solution.py:69
  442.0 186.9 %copy-start.6 = (bf16[24,1536]{1,0:T(8,128)(2,1)S(1)}, bf16[24,1536]{1,0:T(8,128)(2,1)}, u32[]{:S(2)}) copy-start(bf16[24,1536]{1,0:T(8,128)(2,1)} %param.14) | copy-start | bytes 221188
  442.0 186.9 %copy-start.7 = (bf16[24,1536]{1,0:T(8,128)(2,1)S(1)}, bf16[24,1536]{1,0:T(8,128)(2,1)}, u32[]{:S(2)}) copy-start(bf16[24,1536]{1,0:T(8,128)(2,1)} %param.15) | copy-start | bytes 221188
  442.0 193.6 %copy-start.2 = (bf16[512,1536]{1,0:T(8,128)(2,1)S(1)}, bf16[512,1536]{1,0:T(8,128)(2,1)}, u32[]{:S(2)}) copy-start(bf16[512,1536]{1,0:T(8,128)(2,1)} %param.17) | copy-start | bytes 4718596
  630.8 13.9 %all-to-all-start.7 = ((f32[2,1,48]{2,1,0:T(1,128)}), f32[2,1,48]{2,1,0:T(1,128)S(1)}, u32[]{:S(2)}, u32[]{:S(2)}) async-start(f32[2,1,48]{2,1,0:T(1,128)} %broadcast_in_dim.48), calls=%async_computation.9 | async-start | bytes 2048 | tf_op jit(solution)/shard_map/all_to_all | solution.py:15
  635.6 9.2 %copy-start.8 = (f32[1,24,3072]{2,1,0:T(8,128)S(1)}, f32[1,24,3072]{2,1,0:T(8,128)}, u32[]{:S(2)}) copy-start(f32[1,24,3072]{2,1,0:T(8,128)} %reduce-scatter.5.cloned.1.call-done) | copy-start | bytes 884740
Sparse Core Ops, SparseCore 0:
  17.6 114.5 all-gather.1
  412.9 29.0 reduce-scatter.2
  444.4 184.4 reduce-scatter.4
where the time goes:
time: 654 us; the launch traced here: 652 us
  waiting for transfers between devices  380 us (58%)
  matrix products  89.9 us (14%)
  local copies, waits for them, and re-layouts  62 us (9%)
  blocking collectives  43.3 us (7%)
  starting transfers between devices  37.6 us (6%)
  other arithmetic  24.3 us (4%)
  between operations  13.9 us (2%)
    reduce_scatter x1, waiting for transfers between devices, summed_rows(): return lax.psum_scatter(tiles, chips, scatter_dimension=0, tiled=True)[0]  185 us
    all_gather x1, waiting for transfers between devices, sent_together(): lax.all_gather(both, axis, axis=dim, tiled=True)  115 us
    all_to_all x1, blocking collectives, summed_on_arrival(): lax.all_to_all(tiles, axis, split_axis=0, concat_axis=0, tiled=True)  36.9 us
    dot_general x20, matrix products, contract_last(): lax.dot_general(left, right, (((1,), (1,)), ((), ())), preferred_element_...  35.3 us
    all_to_all x5, starting transfers between devices, from_everyone(): lax.all_to_all(jnp.broadcast_to(value[None], (count, *value.shape)), axis...  32.7 us
    reduce_scatter x1, waiting for transfers between devices, summed_rows(): tiles = lax.psum_scatter(tiles, core, scatter_dimension=0, tiled=True)  29.1 us
    dot_general x14, matrix products, contract_first(): lax.dot_general(left, right, (((0,), (0,)), ((), ())), preferred_element_...  27.2 us
    all_to_all x5, waiting for transfers between devices, from_everyone(): lax.all_to_all(jnp.broadcast_to(value[None], (count, *value.shape)), axis...  26.2 us
  transfers between devices with their start and end apart: 9, of which 8 were waited for; matrix products, arithmetic and copies ran while one was open for 4% of the time, Pallas kernels for 0%

commit v1 on v0

--- a/solution.py
+++ b/solution.py
@@ -12,9 +12,7 @@
 
 def from_everyone(value, axis):
     count = lax.axis_size(axis)
-    return lax.all_to_all(
-        jnp.broadcast_to(value[None], (count, *value.shape)), axis, 0, 0, tiled=True
-    )
+    return lax.all_gather(value, axis, axis=0)
 
 
 def of_everyone(value, axis):

time: 654 us -> 669 us (1.023)
  starting transfers between devices: 37.6 us -> 5.35 us
  blocking collectives: 43.3 us -> 61.6 us
  waiting for transfers between devices: 380 us -> 398 us
    all_gather x0 -> x2, waiting for transfers between devices: none -> 52.4 us  [from_everyone(): return lax.all_gather(value, axis, axis=0)]
    all_to_all x5 -> x0, starting transfers between devices: 32.7 us -> none  [from_everyone(): lax.all_to_all(jnp.broadcast_to(value[None], (count, *value.shape)), axis...]
    all_to_all x5 -> x0, waiting for transfers between devices: 26.2 us -> none  [from_everyone(): lax.all_to_all(jnp.broadcast_to(value[None], (count, *value.shape)), axis...]
    unnamed x0 -> x2, blocking collectives: none -> 12.8 us
    all_gather x0 -> x2, blocking collectives: none -> 11.9 us  [from_everyone(): return lax.all_gather(value, axis, axis=0)]
    reduce_scatter x1, waiting for transfers between devices: 185 us -> 175 us  [summed_rows(): return lax.psum_scatter(tiles, chips, scatter_dimension=0, tiled=True)[0]]
  transfers between devices with their start and end apart: 9 -> 6, of which waited for: 8 -> 6; matrix products, arithmetic and copies ran while one was open for 4% -> 4% of each run, Pallas kernels for 0% -> 0%
where the time goes in v1:
time: 669 us; the launch traced here: 666 us
  waiting for transfers between devices  398 us (59%)
  matrix products  95.1 us (14%)
  local copies, waits for them, and re-layouts  66.1 us (10%)
  blocking collectives  61.6 us (9%)
  other arithmetic  25.5 us (4%)
  between operations  14.6 us (2%)
    reduce_scatter x1, waiting for transfers between devices, summed_rows(): return lax.psum_scatter(tiles, chips, scatter_dimension=0, tiled=True)[0]  175 us
    all_gather x1, waiting for transfers between devices, sent_together(): lax.all_gather(both, axis, axis=dim, tiled=True)  114 us
    all_gather x2, waiting for transfers between devices, from_everyone(): return lax.all_gather(value, axis, axis=0)  52.4 us
    all_to_all x1, blocking collectives, summed_on_arrival(): lax.all_to_all(tiles, axis, split_axis=0, concat_axis=0, tiled=True)  36.9 us
    dot_general x20, matrix products, contract_last(): lax.dot_general(left, right, (((1,), (1,)), ((), ())), preferred_element_...  35.3 us
    reduce_scatter x1, waiting for transfers between devices, summed_rows(): tiles = lax.psum_scatter(tiles, core, scatter_dimension=0, tiled=True)  30.5 us
    dot_general x14, matrix products, contract_first(): lax.dot_general(left, right, (((0,), (0,)), ((), ())), preferred_element_...  27.1 us
    all_to_all x1, waiting for transfers between devices, summed_on_arrival(): lax.all_to_all(tiles, axis, split_axis=0, concat_axis=0, tiled=True)  25.8 us
  transfers between devices with their start and end apart: 6, of which 6 were waited for; matrix products, arithmetic and copies ran while one was open for 4% of the time, Pallas kernels for 0%

profile of v1, /device:TPU:6, one launch (start us, length us, event | category | flops | bytes accessed | tf_op | source)
XLA Modules:
  0.0 666.5 jit_solution(3438087110705268449)
XLA Ops:
  10.3 6.4 all-reduce
  19.6 113.9 %all-gather.8.cloned.1.call-done = bf16[1536,3072]{1,0:T(8,128)(2,1)} async-done(((bf16[24,3072]{1,0:T(8,128)(2,1)}), bf16[1536,3072]{1,0:T(8,128)(2,1)}) %all-gather.8.cloned.1.call-update) | async-done | bytes 9437200 | tf_op jit(solution)/shard_map/all_gather | solution.py:37
  133.5 7.2 %fusion.47 = f32[1536,512]{1,0:T(8,128)} fusion(bf16[512,1536]{1,0:T(8,128)(2,1)} %param.11, bf16[1536,3072]{1,0:T(8,128)(2,1)} %all-gather.8.cloned.1.call-done), kind=kOutput, calls=%fused_computation.74 | convolution fusion | flops 2415919104 | bytes 9437184 | tf_op jit(solution)/shard_map/dot_general | solution.py:71
  140.7 5.2 all-to-all-start
  145.9 2.3 copy.73
  150.4 2.3 copy.74
  152.7 2.3 copy.76
  155.0 25.8 %all-to-all-done = f32[2,512,768]{1,2,0:T(8,128)S(1)} async-done(((f32[2,512,768]{1,2,0:T(8,128)}), f32[2,512,768]{1,2,0:T(8,128)S(1)}, u32[]{:S(2)}, u32[]{:S(2)}) %all-to-all-start) | async-done | bytes 3145760 | tf_op jit(solution)/shard_map/all_to_all | solution.py:47
  182.2 2.3 copy.77
  184.6 17.6 %while.24 = (s32[]{:T(128)}, bf16[6,512,128]{1,2,0:T(8,128)(2,1)S(1)}, bf16[6,512,128]{2,1,0:T(8,128)(2,1)}, bf16[6,512,128]{2,1,0:T(8,128)(2,1)}, bf16[6,512,128]{2,1,0:T(8,128)(2,1)}, /*index=5*/s32[]{:T(128)}) while((s32[]{:T(128)}, bf16[6,512,128]{1,2,0:T(8,128)(2,1)S(1)}, bf16[6,512,128]{2,1,0:T(8,128)(2,1)}, ...), condition=%wide.region_7.8_spmd, body=%wide.region_4.7_spmd.sunk | while | flops 136641536 | bytes 4205653 | solution.py:145
  203.5 29.2 %all-gather.10.cloned.1.call-done = bf16[2,512,768]{2,1,0:T(8,128)(2,1)} async-done(((bf16[1,512,768]{2,1,0:T(8,128)(2,1)}), bf16[2,512,768]{2,1,0:T(8,128)(2,1)}) %all-gather.10.cloned.1.call-update) | async-done | bytes 1572880 | tf_op jit(solution)/shard_map/all_gather | solution.py:15
  232.7 2.6 copy.80
  235.3 8.4 %fusion.54 = (f32[512]{0:T(512)S(1)}, f32[512]{0:T(512)S(1)}, f32[512]{0:T(512)S(1)}, f32[512]{0:T(512)S(1)}, f32[512]{0:T(512)S(1)}, /*index=5*/f32[512]{0:T(512)S(1)}, f32[512,1536]{1,0:T(8,128)S(1)}) fusion(bf16[512,1536]{1,0:T(8,128)(2,1)} %param.17, f32[1536]{0:T(1024)S(1)} %copy-done.7, f32[1536]{0:T(1024)S(1)} %get-tuple-element.206, ...), kind=kOutput, calls=%fused_computation.79 | convolution fusion | flops 2430858240 | bytes 12625920 | tf_op jit(solution)/shard_map/dot_general | solution.py:147
  243.7 5.9 all-gather.1
  249.6 6.0 all-gather.2
  255.7 4.4 multiply_convert_fusion.1
  260.1 5.1 fusion.41
  265.4 36.9 %all_to_all.10 = f32[2,512,768]{2,1,0:T(8,128)S(1)} all-to-all(f32[2,512,768]{2,1,0:T(8,128)S(1)} %bitcast.141), channel_id=1, replica_groups=mesh['fsdp_0'=2,'fsdp_1'=4,'fsdp_2'=4,'fsdp_3'=2,'grp'=2] {'grp'}, dimensions={0} | all-to-all | bytes 6291456 | tf_op jit(solution)/shard_map/all_to_all | solution.py:47
  303.6 2.3 copy.83
  307.0 47.0 %while.25 = (s32[]{:T(128)}, bf16[6,512,128]{1,2,0:T(8,128)(2,1)S(1)}, bf16[6,512,128]{1,2,0:T(8,128)(2,1)S(1)}, bf16[6,512,128]{1,2,0:T(8,128)(2,1)}, bf16[6,51...) while((s32[]{:T(128)}, ...), condition=%wide.region_21.22_spmd, body=%wide.region_17.21_spmd.sunk | while | flops 340589056 | bytes 11821177 | solution.py:186
  354.0 2.3 copy.89
  356.3 8.2 %fusion.86 = f32[1536,1536]{0,1:T(8,128)} fusion(bf16[512,1536]{0,1:T(8,128)(2,1)} %bitcast.152, bf16[512,1536]{1,0:T(8,128)(2,1)} %copy-done.4), kind=kOutput, calls=%fused_computation.133 | convolution fusion | flops 2415919104 | bytes 12582912 | tf_op jit(solution)/shard_map/dot_general | solution.py:77
  364.5 23.2 %all-gather.12.cloned.1.call-done = bf16[2,512,768]{2,1,0:T(8,128)(2,1)} async-done(((bf16[1,512,768]{2,1,0:T(8,128)(2,1)}), bf16[2,512,768]{2,1,0:T(8,128)(2,1)}) %all-gather.12.cloned.1.call-update) | async-done | bytes 1572880 | tf_op jit(solution)/shard_map/all_gather | solution.py:15
  387.7 2.6 copy.90
  390.3 4.2 fusion.85
  394.6 7.2 %pad_maximum_fusion = f32[1536,3072]{0,1:T(8,128)} fusion(f32[1536,1536]{0,1:T(8,128)S(1)} %copy-done, f32[1536,1536]{0,1:T(8,128)S(1)} %fusion.85), kind=kLoop, calls=%fused_computation.57 | loop fusion | flops 4718592 | bytes 37748736 | tf_op jit(solution)/shard_map/concatenate | solution.py:194
  401.7 18.7 %copy.93 = f32[1536,3072]{1,0:T(8,128)} copy(f32[1536,3072]{0,1:T(8,128)} %pad_maximum_fusion) | data formatting | bytes 37748736 | tf_op jit(solution)/shard_map/concatenate | solution.py:194
  420.4 12.8 %copy.94 = f32[2,32,24,3072]{3,2,1,0:T(8,128)} copy(f32[2,32,24,3072]{3,2,0,1:T(8,128)} %bitcast.140) | data formatting | bytes 37748736 | tf_op jit(solution)/shard_map/transpose | solution.py:65
  433.3 30.5 %reduce-scatter.3.cloned.1.call-done = f32[32,24,3072]{2,1,0:T(8,128)} async-done(((f32[64,24,3072]{2,1,0:T(8,128)}), f32[32,24,3072]{2,1,0:T(8,128)}) %reduce-scatter.3.cloned.1.call-update) | async-done | bytes 9437200 | tf_op jit(solution)/shard_map/reduce_scatter | solution.py:66
  466.2 9.1 %fusion.62 = bf16[512,1536]{1,0:T(8,128)(2,1)} fusion(bf16[512,1536]{0,1:T(8,128)(2,1)} %bitcast.154, bf16[1536,3072]{1,0:T(8,128)(2,1)} %all-gather.8.cloned.1.call-done, bf16[512,1536]{1,0:T(8,128)(2,1)S(1)} %copy-done.2, f32[512]{0:T(512)S(1)} %get-tuple-element.192, f32[1536]{0:T(1024)S(1)} %get-tuple-element.209, f32[512]{0:T(512)S(1)} %get-tuple-element.207, ...), kind=kOutput, calls=%fused_computation.90 | convolution fusion | flops 2426929152 | bytes 14174208 | tf_op jit(solution)/shard_map/dot_general | solution.py:191
  475.3 174.8 %reduce-scatter.5.cloned.1.call-done = f32[1,24,3072]{2,1,0:T(8,128)} async-done(((f32[32,24,3072]{2,1,0:T(8,128)}), f32[1,24,3072]{2,1,0:T(8,128)}) %reduce-scatter.5.cloned.1.call-update) | async-done | bytes 294928 | tf_op jit(solution)/shard_map/reduce_scatter | solution.py:67
  651.5 6.4 all-reduce.1
  (164 shorter events, 82.8 us)
Async XLA Ops:
  7.2 126.4 %all-gather.8.cloned.1.call-start = ((), (), s32[]{:S(2)}) async-start(), calls=%async_computation.4 | async-start | bytes 9584640 | tf_op jit(solution)/shard_map/all_gather | solution.py:37
  140.7 40.2 %all-to-all-start = ((f32[2,512,768]{1,2,0:T(8,128)}), f32[2,512,768]{1,2,0:T(8,128)S(1)}, u32[]{:S(2)}, u32[]{:S(2)}) async-start(f32[2,512,768]{1,2,0:T(8,128)} %bitcast.142), calls=%async_computation | async-start | bytes 6291456 | tf_op jit(solution)/shard_map/all_to_all | solution.py:47
  145.9 86.8 %all-gather.10.cloned.1.call-start = ((), (), s32[]{:S(2)}) async-start(), calls=%async_computation.5 | async-start | bytes 2359296 | tf_op jit(solution)/shard_map/all_gather | solution.py:15
  184.6 18.8 %copy-start.7 = (f32[1536]{0:T(1024)S(1)}, f32[1536]{0:T(1024)}, u32[]{:S(2)}) copy-start(f32[1536]{0:T(1024)} %param.16) | copy-start | bytes 18436
  203.4 184.3 %all-gather.12.cloned.1.call-start = ((), (), s32[]{:S(2)}) async-start(), calls=%async_computation.6 | async-start | bytes 2359296 | tf_op jit(solution)/shard_map/all_gather | solution.py:15
  243.7 16.4 %copy-start.1 = (f32[512,1536]{1,0:T(8,128)}, f32[512,1536]{1,0:T(8,128)S(1)}, u32[]{:S(2)}) copy-start(f32[512,1536]{1,0:T(8,128)S(1)} %get-tuple-element.215) | copy-start | bytes 9437188
  260.1 5.1 copy-start.4
  356.3 107.6 %reduce-scatter.3.cloned.1.call-start = ((), (), s32[]{:S(2)}) async-start(), calls=%async_computation.7 | async-start | bytes 28311552 | tf_op jit(solution)/shard_map/reduce_scatter | solution.py:66
  364.5 25.8 %copy-start.3 = (bf16[512,1536]{1,0:T(8,128)(2,1)S(1)}, bf16[512,1536]{1,0:T(8,128)(2,1)}, u32[]{:S(2)}) copy-start(bf16[512,1536]{1,0:T(8,128)(2,1)} %param.11) | copy-start | bytes 4718596
  390.3 4.3 copy-start
  433.3 216.8 %reduce-scatter.5.cloned.1.call-start = ((), (), s32[]{:S(2)}) async-start(), calls=%async_computation.8 | async-start | bytes 9732096 | tf_op jit(solution)/shard_map/reduce_scatter | solution.py:67
  463.9 2.3 copy-start.2
  466.2 183.9 %copy-start.5 = (bf16[24,1536]{1,0:T(8,128)(2,1)S(1)}, bf16[24,1536]{1,0:T(8,128)(2,1)}, u32[]{:S(2)}) copy-start(bf16[24,1536]{1,0:T(8,128)(2,1)} %param.14) | copy-start | bytes 221188
  466.2 183.9 %copy-start.6 = (bf16[24,1536]{1,0:T(8,128)(2,1)S(1)}, bf16[24,1536]{1,0:T(8,128)(2,1)}, u32[]{:S(2)}) copy-start(bf16[24,1536]{1,0:T(8,128)(2,1)} %param.15) | copy-start | bytes 221188
Sparse Core Ops, SparseCore 0:
  19.7 113.7 all-gather.7
  203.5 29.1 all-gather.9
  356.4 31.2 all-gather.11
  433.4 30.4 reduce-scatter.2
  466.1 183.9 reduce-scatter.4
